TPU v7x, 32 devices: a whole 2x2x4 slice. The times are simulated.
32 devices in a mesh: dp: 8 (over z, y), comp: 4 (over x, core).
Axes of the slice: x: 2, y: 2, z: 4, core: 2. Of those that a mesh axis runs over, the one named last changes fastest.
Arguments:
- points: float32 [8192, 64], P('dp'), may hold values from -36 to 36
- means: float32 [256, 64], P('comp'), may hold values from -6 to 6
- whiten: float32 [256, 64, 64], P('comp'), may hold values from -0.25 to 2, as said below
- log_weight: float32 [256], P('comp'), may hold values from -4 to 4
Outputs:
- new_means: float32 [256, 64], P('comp')
- new_whiten: float32 [256, 64, 64], P('comp')
- new_log_weight: float32 [256], P('comp')
- point_loglik: float32 [8192], P('dp')
Inputs may be any that keep to these rules, and one draw needn't show every extreme that they name: Each whiten[k] is lower triangular with diagonal entries between 0.5 and 2.
All inputs are finite; a program needn't handle non-finite values.
Results may differ from a plain program's by a relative error of at most 0.0003.
Values sent between devices are 32-bit elements; how exact they have to be, the bound alone decides.
A program may use at most 64 MiB of HBM per device.

v0:
```python
import math
import jax
import jax.numpy as jnp
from jax import lax
from jax.sharding import PartitionSpec as P

K = 256
HIGH = lax.Precision.HIGHEST


def refit_params(square, sums, counts, width, total_points):
    grown = counts + 1.0
    centre = sums / grown[:, None]
    eye = jnp.eye(width, dtype=jnp.float32)
    cov = (square - sums[:, :, None] * sums[:, None, :] / grown[:, None, None] + eye[None]) / grown[
        :, None, None
    ]
    chol = jnp.linalg.cholesky(cov)
    factor = lax.linalg.triangular_solve(
        chol, jnp.broadcast_to(eye, chol.shape), left_side=True, lower=True
    )
    weight = jnp.log(grown / (total_points + K))
    return (centre, factor, weight)


def body(points, means, whiten, log_weight):
    count_rows, width = points.shape
    local = means.shape[0]
    block = min(512, count_rows)
    blocks = count_rows // block
    stacked = whiten.reshape(local * width, width)
    offset = jnp.einsum("ked,kd->ke", whiten, means, precision=HIGH).reshape(local * width, 1)
    logdet = jnp.sum(jnp.log(jnp.diagonal(whiten, axis1=1, axis2=2)), axis=1)
    const = log_weight + logdet - 0.5 * width * math.log(2.0 * math.pi)
    tiles = points.reshape(blocks, block, width)

    def score(tile):
        projected = (
            lax.dot_general(stacked, tile, (((1,), (1,)), ((), ())), precision=HIGH) - offset
        )
        distance = jnp.sum((projected * projected).reshape(local, width, block), axis=1)
        return const[:, None] - 0.5 * distance

    logp = lax.map(score, tiles)
    peak = jnp.max(logp, axis=1)
    peak = lax.pmax(peak, "comp")
    partial_total = jnp.sum(jnp.exp(logp - peak[:, None, :]), axis=1)
    total = lax.psum(partial_total, "comp")
    lse = peak + jnp.log(total)
    resp = jnp.exp(logp - lse[:, None, :])

    def accumulate(carry, pieces):
        tile, weight = pieces
        outer = (tile[:, :, None] * tile[:, None, :]).reshape(block, width * width)
        scatter = carry[0] + jnp.dot(weight, outer, precision=HIGH)
        sums = carry[1] + jnp.dot(weight, tile, precision=HIGH)
        counts = carry[2] + jnp.sum(weight, axis=1)
        return ((scatter, sums, counts), None)

    columns = width * width
    start = (
        jnp.zeros((local, columns), jnp.float32),
        jnp.zeros((local, width), jnp.float32),
        jnp.zeros((local,), jnp.float32),
    )
    (scatter, sums, counts), unused = lax.scan(accumulate, start, (tiles, resp))
    total_points = count_rows * lax.axis_size("dp")
    scatter, sums, counts = (
        lax.psum_scatter(scatter, "dp", scatter_dimension=0, tiled=True),
        lax.psum_scatter(sums, "dp", scatter_dimension=0, tiled=True),
        lax.psum_scatter(counts, "dp", scatter_dimension=0, tiled=True),
    )
    centre, factor, weight = refit_params(
        scatter.reshape(scatter.shape[0], width, width), sums, counts, width, total_points
    )
    centre, factor, weight = (
        lax.all_gather(centre, "dp", axis=0, tiled=True),
        lax.all_gather(factor, "dp", axis=0, tiled=True),
        lax.all_gather(weight, "dp", axis=0, tiled=True),
    )
    return (centre, factor, weight, (lse / width).reshape(count_rows))


def solution(mesh):
    in_specs = (P("dp", None), P("comp", None), P("comp", None, None), P("comp"))
    out_specs = (P("comp", None), P("comp", None, None), P("comp"), P("dp"))
    return jax.shard_map(body, mesh=mesh, in_specs=in_specs, out_specs=out_specs, check_vma=False)
```

profile of v0, /device:TPU:0, one launch (start us, length us, event | category | flops | bytes accessed | tf_op | source)
XLA Modules:
  0.0 330.3 jit_solution(15399564940060556085)
XLA Ops:
  7.3 1.2 reshape.97
  8.4 2.4 copy.41
  10.8 0.9 gather_fusion
  11.7 4.9 %fusion.15 = f32[64,1,64]{2,1,0:T(1,128)S(1)} fusion(f32[64,64,64]{2,1,0:T(8,128)} %param.10, f32[64,64,1]{1,2,0:T(1,128)S(1)} %bitcast.74), kind=kOutput, calls=%fused_computation.45 | convolution fusion | flops 3145728 | bytes 1081344 | tf_op jit(solution)/shard_map/ked,kd->ke/dot_general | solution.py:32
  17.4 50.3 %while.25 = (s32[]{:T(128)}, f32[2,64,512]{2,1,0:T(8,128)}, f32[64]{0:T(128)S(1)}, f32[2,512,64]{1,0,2:T(2,128)S(1)}, f32[4096,64]{1,0:T(8,128)}, /*index=5*/f32[4096,1]{0,1:T(1,128)S(1)}, s32[]{:T(128)}) while((s32[]{:T(128)}, f32[2,64,512]{2,1,0:T(8,128)}, f32[64]{0:T(128)S(1)}, f32[2,512,64]{1,0,2:T(2,128)S(1)}, f32[4096,64]{1,0:T(8,128)}, ...), condition=%wide.region_3.4_spmd, body=%wide.region_1.3_spmd.sunk | while | flops 1616936960 | bytes 37765772 | solution.py:44
  17.7 10.3 %multiply_bitcast_fusion.3 = f32[4096,512]{0,1:T(8,128)} fusion(f32[4096,64]{1,0:T(8,128)} %get-tuple-element.263, f32[4096]{0:T(1024)S(1)} %bitcast.78, f32[1,512,64]{2,1,0:T(8,128)S(1)} %copy.63), kind=kOutput, calls=%fused_computation.2.clone.1 | convolution fusion | flops 1614807040 | bytes 9584640 | tf_op jit(solution)/shard_map/while/body/eval_jaxpr/dot_general | solution.py:39
  28.0 9.0 %copy.64 = f32[4096,512]{1,0:T(8,128)} copy(f32[4096,512]{0,1:T(8,128)} %multiply_bitcast_fusion.3) | data formatting | bytes 16777216 | tf_op jit(solution)/shard_map/while/body/eval_jaxpr/mul | solution.py:41
  37.0 4.8 %bitcast_reduce_fusion.2 = f32[64,512]{1,0:T(8,128)S(1)} fusion(f32[4096,512]{1,0:T(8,128)} %copy.64), kind=kLoop, calls=%fused_computation.1.clone.1 | loop fusion | flops 2064384 | bytes 8519680 | tf_op jit(solution)/shard_map/while/body/eval_jaxpr/reduce_sum | solution.py:41
  42.8 10.3 %multiply_bitcast_fusion.3 = f32[4096,512]{0,1:T(8,128)} fusion(f32[4096,64]{1,0:T(8,128)} %get-tuple-element.263, f32[4096]{0:T(1024)S(1)} %bitcast.78, f32[1,512,64]{2,1,0:T(8,128)S(1)} %copy.63), kind=kOutput, calls=%fused_computation.2.clone.1 | convolution fusion | flops 1614807040 | bytes 9584640 | tf_op jit(solution)/shard_map/while/body/eval_jaxpr/dot_general | solution.py:39
  53.2 9.0 %copy.64 = f32[4096,512]{1,0:T(8,128)} copy(f32[4096,512]{0,1:T(8,128)} %multiply_bitcast_fusion.3) | data formatting | bytes 16777216 | tf_op jit(solution)/shard_map/while/body/eval_jaxpr/mul | solution.py:41
  62.1 4.8 %bitcast_reduce_fusion.2 = f32[64,512]{1,0:T(8,128)S(1)} fusion(f32[4096,512]{1,0:T(8,128)} %copy.64), kind=kLoop, calls=%fused_computation.1.clone.1 | loop fusion | flops 2064384 | bytes 8519680 | tf_op jit(solution)/shard_map/while/body/eval_jaxpr/reduce_sum | solution.py:41
  67.7 1.0 reduce_max.9
  68.7 8.4 %pmax.7 = f32[2,512]{1,0:T(2,128)S(1)} all-reduce(f32[2,512]{1,0:T(2,128)S(1)} %reduce_max.9), channel_id=1, replica_groups=mesh['dp'=8,'comp'=4] {'comp'}, use_global_device_ids=true, to_apply=%region_5.6 | all-reduce | flops 1024 | bytes 8192 | tf_op jit(solution)/shard_map/pmax | solution.py:46
  77.1 1.0 exponential_reduce_fusion
  78.1 5.8 %psum.7 = f32[2,512]{1,0:T(2,128)S(1)} all-reduce(f32[2,512]{1,0:T(2,128)S(1)} %exponential_reduce_fusion), channel_id=1, replica_groups=mesh['dp'=8,'comp'=4] {'comp'}, use_global_device_ids=true, to_apply=%region_7.8 | all-reduce | flops 1024 | bytes 8192 | tf_op jit(solution)/shard_map/psum | solution.py:48
  83.9 1.0 subtract_exponential_fusion
  84.9 30.5 %while.26 = (s32[]{:T(128)}, f32[64,4096]{1,0:T(8,128)S(1)}, f32[64,64]{1,0:T(8,128)S(1)}, f32[64]{0:T(128)S(1)}, f32[2,64,512]{2,1,0:T(8,128)S(1)}, /*index=5*/f32[2,512,64]{1,0,2:T(2,128)S(1)}, s32[]{:T(128)}, s32[]{:T(128)}) while((s32[]{:T(128)}, f32[64,4096]{1,0:T(8,128)S(1)}, f32[64,64]{1,0:T(8,128)S(1)}, ...), condition=%wide.region_10.11_spmd.clone, body=%wide.region_8.10_spmd.clone.sunk | while | flops 1638441088 | bytes 20104304 | solution.py:66
  85.0 4.3 %broadcast_multiply_fusion.2 = f32[512,64,64]{0,2,1:T(8,128)} fusion(f32[512,64]{0,1:T(8,128)S(1)} %bitcast.77), kind=kLoop, calls=%fused_computation.8.clone.1 | loop fusion | flops 2097152 | bytes 8519680 | tf_op jit(solution)/shard_map/while/body/eval_jaxpr/mul | solution.py:54
  89.4 10.3 %convolution_add_fusion.4 = f32[64,4096]{1,0:T(8,128)S(1)} fusion(f32[512,4096]{0,1:T(8,128)} %bitcast.75, f32[64,4096]{1,0:T(8,128)S(1)} %get-tuple-element.275, pred[]{:T(512)S(6)} %compare.11, f32[2,64,512]{2,1,0:T(8,128)S(1)} %get-tuple-element.286, s32[]{:T(128)} %get-tuple-element.274), kind=kOutput, calls=%fused_computation.7.clone.1 | convolution fusion | flops 1611137024 | bytes 10616837 | tf_op jit(solution)/shard_map/while/body/eval_jaxpr/dot_general | solution.py:55
  100.3 4.3 %broadcast_multiply_fusion.2 = f32[512,64,64]{0,2,1:T(8,128)} fusion(f32[512,64]{0,1:T(8,128)S(1)} %bitcast.77), kind=kLoop, calls=%fused_computation.8.clone.1 | loop fusion | flops 2097152 | bytes 8519680 | tf_op jit(solution)/shard_map/while/body/eval_jaxpr/mul | solution.py:54
  104.6 10.3 %convolution_add_fusion.4 = f32[64,4096]{1,0:T(8,128)S(1)} fusion(f32[512,4096]{0,1:T(8,128)} %bitcast.75, f32[64,4096]{1,0:T(8,128)S(1)} %get-tuple-element.275, pred[]{:T(512)S(6)} %compare.11, f32[2,64,512]{2,1,0:T(8,128)S(1)} %get-tuple-element.286, s32[]{:T(128)} %get-tuple-element.274), kind=kOutput, calls=%fused_computation.7.clone.1 | convolution fusion | flops 1611137024 | bytes 10616837 | tf_op jit(solution)/shard_map/while/body/eval_jaxpr/dot_general | solution.py:55
  115.4 1.0 copy-done.1
  118.4 21.9 %all-reduce.2 = f32[64]{0:T(128)S(1)} all-reduce(f32[64]{0:T(128)S(1)} %get-tuple-element.72), channel_id=3, replica_groups=mesh['dp'=8,'comp'=4] {'dp'}, use_global_device_ids=true, to_apply=%region_12.13.clone | all-reduce | flops 64 | bytes 512
  140.5 33.9 %all-reduce.3 = (f32[64,64]{1,0:T(8,128)S(1)}, f32[64]{0:T(128)}) all-reduce(f32[64,64]{1,0:T(8,128)S(1)} %get-tuple-element.71, f32[64]{0:T(128)S(1)} %get-tuple-element.167), channel_id=2, replica_groups=mesh['dp'=8,'comp'=4] {'dp'}, use_global_device_ids=true, to_apply=%region_11.12.clone | all-reduce | flops 4160 | bytes 33280
  174.5 7.4 %reduce-scatter.2.cloned.1.call-done = f32[8,4096]{1,0:T(8,128)} async-done(((f32[64,4096]{1,0:T(8,128)}), f32[8,4096]{1,0:T(8,128)}) %reduce-scatter.2.cloned.1.call-update) | async-done | bytes 131088 | tf_op jit(solution)/shard_map/reduce_scatter | solution.py:69
  181.9 1.0 reshape.100
  183.5 46.9 %custom-call.7 = f32[8,64,64]{2,1,0:T(8,128)S(1)} custom-call(f32[8,64,64]{2,1,0:T(8,128)S(1)} %fusion.11), custom_call_target="Cholesky" | custom-call | tf_op jit(solution)/shard_map/jit(cholesky)/cholesky | solution.py:18
  230.7 39.3 %custom-call.8 = f32[8,1,64,64]{2,3,1,0:T(8,128)S(1)} custom-call(f32[8,1,64,64]{3,2,1,0:T(8,128)S(1)} %select_bitcast_fusion), custom_call_target="InvertDiagBlocksLowerTriangular" | custom-call | tf_op jit(solution)/shard_map/triangular_solve | solution.py:19
  270.0 1.3 fusion.9
  271.3 30.9 %all_gather.9 = f32[64,64]{1,0:T(8,128)S(1)} all-gather(f32[8,64]{1,0:T(8,128)S(1)} %get-tuple-element.165), channel_id=1, replica_groups=mesh['dp'=8,'comp'=4] {'dp'}, dimensions={0}, use_global_device_ids=true | all-gather | bytes 18432 | tf_op jit(solution)/shard_map/all_gather | solution.py:77
  302.8 16.9 %all-gather.2.cloned.1.call-done = f32[64,64,64]{2,1,0:T(8,128)} async-done(((f32[8,64,64]{2,1,0:T(8,128)}), f32[64,64,64]{2,1,0:T(8,128)}) %all-gather.2.cloned.1.call-update) | async-done | bytes 1048592 | tf_op jit(solution)/shard_map/all_gather | solution.py:78
  320.3 3.2 copy.90
  (59 shorter events, 7.0 us)
Async XLA Ops:
  7.2 4.6 %copy-start = (f32[64,64]{1,0:T(8,128)S(1)}, f32[64,64]{1,0:T(8,128)}, u32[]{:S(2)}) copy-start(f32[64,64]{1,0:T(8,128)} %param.9) | copy-start | bytes 49156
  7.2 174.7 %reduce-scatter.2.cloned.1.call-start = ((), (), s32[]{:S(2)}) async-start(), calls=%async_computation.1 | async-start | bytes 1179648 | tf_op jit(solution)/shard_map/reduce_scatter | solution.py:69
  37.0 4.8 %copy-start.2 = (f32[2,64,512]{2,1,0:T(8,128)S(1)}, f32[2,64,512]{2,1,0:T(8,128)}, u32[]{:S(2)}) copy-start(f32[2,64,512]{2,1,0:T(8,128)} %get-tuple-element.253) | copy-start | bytes 786436 | tf_op jit(solution)/shard_map/while
  41.9 0.7 copy-start.3
  62.1 4.8 %copy-start.2 = (f32[2,64,512]{2,1,0:T(8,128)S(1)}, f32[2,64,512]{2,1,0:T(8,128)}, u32[]{:S(2)}) copy-start(f32[2,64,512]{2,1,0:T(8,128)} %get-tuple-element.253) | copy-start | bytes 786436 | tf_op jit(solution)/shard_map/while
  67.0 0.7 copy-start.3
  84.9 31.7 %copy-start.4 = (u32[32]{0:T(128)S(1)}, u32[32]{0:T(128)}, u32[]{:S(2)}) copy-start(u32[32]{0:T(128)} %constant.106) | copy-start | bytes 388
  115.4 1.0 copy-start.1
  116.4 203.3 %all-gather.2.cloned.1.call-start = ((), (), s32[]{:S(2)}) async-start(), calls=%async_computation.2 | async-start | bytes 2359296 | tf_op jit(solution)/shard_map/all_gather | solution.py:78
Sparse Core Ops, SparseCore 0:
  116.5 65.3 reduce-scatter.1
  271.5 48.1 all-gather.1
where the time goes:
time: 331 us; the launch traced here: 330 us
  other arithmetic  109 us (33%)
  blocking collectives  101 us (31%)
  matrix products  48.1 us (15%)
  local copies, waits for them, and re-layouts  31.9 us (10%)
  waiting for transfers between devices  24.3 us (7%)
  between operations  15.5 us (5%)
    unnamed x2, blocking collectives  55.8 us
    another operation x4, other arithmetic, refit_params(): chol = jnp.linalg.cholesky(cov)  47.1 us
    another operation x3, other arithmetic, refit_params(): lax.linalg.triangular_solve(chol, jnp.broadcast_to(eye, chol.shape), left...  39.4 us
    all_gather x1, blocking collectives, body(): lax.all_gather(centre, 'dp', axis=0, tiled=True)  30.9 us
    dot_general x2, matrix products, accumulate(): scatter = carry[0] + jnp.dot(weight, outer, precision=HIGH)  20.7 us
    dot_general x2, matrix products, score(): lax.dot_general(stacked, tile, (((1,), (1,)), ((), ())), precision=HIGH)  20.6 us
    mul x2, local copies, waits for them, and re-layouts, score(): projected * projected  18 us
    all_gather x1, waiting for transfers between devices, body(): lax.all_gather(factor, 'dp', axis=0, tiled=True)  16.9 us
  transfers between devices with their start and end apart: 2, of which 2 were waited for; matrix products, arithmetic and copies ran while one was open for 0% of the time, Pallas kernels for 0%

commit v1 on v0

--- a/solution.py
+++ b/solution.py
@@ -6,6 +6,18 @@
 
 K = 256
 HIGH = lax.Precision.HIGHEST
+
+
+def collect(x, axis, dim):
+    ways, here, hop = (lax.axis_size(axis), lax.axis_index(axis), x.shape[dim])
+    line, have = (x, 1)
+    while have < ways:
+        line = jnp.concatenate(
+            [line, lax.ppermute(line, axis, [(d, (d - have) % ways) for d in range(ways)])],
+            axis=dim,
+        )
+        have = 2 * have
+    return jnp.roll(line, here * hop, axis=dim)
 
 
 def refit_params(square, sums, counts, width, total_points):
@@ -75,7 +87,7 @@
     )
     centre, factor, weight = (
         lax.all_gather(centre, "dp", axis=0, tiled=True),
-        lax.all_gather(factor, "dp", axis=0, tiled=True),
+        collect(factor, "dp", 0),
         lax.all_gather(weight, "dp", axis=0, tiled=True),
     )
     return (centre, factor, weight, (lse / width).reshape(count_rows))

time: 331 us -> 377 us (1.14)
  blocking collectives: 101 us -> 137 us
  local copies, waits for them, and re-layouts: 31.9 us -> 42.8 us
  starting transfers between devices: 0.08 us -> 6.93 us
  matrix products: 48.1 us -> 44.1 us
  waiting for transfers between devices: 24.3 us -> 20.3 us
    all_gather x1, blocking collectives: 30.9 us -> 66.6 us  [body(): lax.all_gather(centre, 'dp', axis=0, tiled=True)]
    all_gather x1 -> x0, waiting for transfers between devices: 16.9 us -> none  [body(): lax.all_gather(factor, 'dp', axis=0, tiled=True)]
    ppermute x0 -> x3, waiting for transfers between devices: none -> 13.1 us  [collect(): lax.ppermute(line, axis, [(d, (d - have) % ways) for d in range(ways)])]
    ppermute x0 -> x3, starting transfers between devices: none -> 6.89 us  [collect(): lax.ppermute(line, axis, [(d, (d - have) % ways) for d in range(ways)])]
    unnamed x11 -> x20, local copies, waits for them, and re-layouts: 8.31 us -> 11.1 us
  transfers between devices with their start and end apart: 2 -> 4, of which waited for: 2 -> 3; matrix products, arithmetic and copies ran while one was open for 0% -> 1% of each run, Pallas kernels for 0% -> 0%
where the time goes in v1:
time: 377 us
  blocking collectives  137 us (36%)
  other arithmetic  110 us (29%)
  matrix products  44.1 us (12%)
  local copies, waits for them, and re-layouts  42.8 us (11%)
  waiting for transfers between devices  20.3 us (5%)
  between operations  15.6 us (4%)
  starting transfers between devices  6.93 us (2%)
    all_gather x1, blocking collectives, body(): lax.all_gather(centre, 'dp', axis=0, tiled=True)  66.6 us
    unnamed x2, blocking collectives  56 us
    another operation x4, other arithmetic, refit_params(): chol = jnp.linalg.cholesky(cov)  47.1 us
    another operation x3, other arithmetic, refit_params(): lax.linalg.triangular_solve(chol, jnp.broadcast_to(eye, chol.shape), left...  39.4 us
    dot_general x2, matrix products, accumulate(): scatter = carry[0] + jnp.dot(weight, outer, precision=HIGH)  20.7 us
    dot_general x2, matrix products, score(): lax.dot_general(stacked, tile, (((1,), (1,)), ((), ())), precision=HIGH)  18.2 us
    mul x2, local copies, waits for them, and re-layouts, score(): projected * projected  18 us
    ppermute x3, waiting for transfers between devices, collect(): lax.ppermute(line, axis, [(d, (d - have) % ways) for d in range(ways)])  13.1 us
  transfers between devices with their start and end apart: 4, of which 3 were waited for; matrix products, arithmetic and copies ran while one was open for 1% of the time, Pallas kernels for 0%

profile of v1, /device:TPU:0, one launch (start us, length us, event | category | flops | bytes accessed | tf_op | source)
XLA Modules:
  0.0 376.7 jit_solution(1718755375665119143)
XLA Ops:
  7.3 1.3 reshape.97
  8.6 3.3 copy.41
  11.9 1.6 gather_fusion
  13.6 3.3 fusion.15
  17.0 52.2 %while.25 = (s32[]{:T(128)}, f32[2,64,512]{2,1,0:T(8,128)}, f32[64]{0:T(128)S(1)}, f32[2,512,64]{1,0,2:T(2,128)S(1)}, f32[4096,64]{1,0:T(8,128)S(1)}, /*index=5*/f32[4096,1]{0,1:T(1,128)S(1)}, s32[]{:T(128)}) while((s32[]{:T(128)}, f32[2,64,512]{2,1,0:T(8,128)}, f32[64]{0:T(128)S(1)}, f32[2,512,64]{1,0,2:T(2,128)S(1)}, ...), condition=%wide.region_3.4_spmd, body=%wide.region_1.3_spmd.sunk | while | flops 1616936960 | bytes 37766024 | solution.py:56
  19.5 9.1 %multiply_bitcast_fusion.3 = f32[4096,512]{0,1:T(8,128)} fusion(f32[4096,64]{1,0:T(8,128)S(1)} %get-tuple-element.265, f32[4096]{0:T(1024)S(1)} %bitcast.80, f32[1,512,64]{2,1,0:T(8,128)S(1)} %copy.63), kind=kOutput, calls=%fused_computation.2.clone.1 | convolution fusion | flops 1614807040 | bytes 9584640 | tf_op jit(solution)/shard_map/while/body/eval_jaxpr/dot_general | solution.py:51
  28.6 9.0 %copy.64 = f32[4096,512]{1,0:T(8,128)} copy(f32[4096,512]{0,1:T(8,128)} %multiply_bitcast_fusion.3) | data formatting | bytes 16777216 | tf_op jit(solution)/shard_map/while/body/eval_jaxpr/mul | solution.py:53
  37.6 4.8 %bitcast_reduce_fusion.2 = f32[64,512]{1,0:T(8,128)S(1)} fusion(f32[4096,512]{1,0:T(8,128)} %copy.64), kind=kLoop, calls=%fused_computation.1.clone.1 | loop fusion | flops 2064384 | bytes 8519680 | tf_op jit(solution)/shard_map/while/body/eval_jaxpr/reduce_sum | solution.py:53
  45.6 9.1 %multiply_bitcast_fusion.3 = f32[4096,512]{0,1:T(8,128)} fusion(f32[4096,64]{1,0:T(8,128)S(1)} %get-tuple-element.265, f32[4096]{0:T(1024)S(1)} %bitcast.80, f32[1,512,64]{2,1,0:T(8,128)S(1)} %copy.63), kind=kOutput, calls=%fused_computation.2.clone.1 | convolution fusion | flops 1614807040 | bytes 9584640 | tf_op jit(solution)/shard_map/while/body/eval_jaxpr/dot_general | solution.py:51
  54.7 9.0 %copy.64 = f32[4096,512]{1,0:T(8,128)} copy(f32[4096,512]{0,1:T(8,128)} %multiply_bitcast_fusion.3) | data formatting | bytes 16777216 | tf_op jit(solution)/shard_map/while/body/eval_jaxpr/mul | solution.py:53
  63.7 4.8 %bitcast_reduce_fusion.2 = f32[64,512]{1,0:T(8,128)S(1)} fusion(f32[4096,512]{1,0:T(8,128)} %copy.64), kind=kLoop, calls=%fused_computation.1.clone.1 | loop fusion | flops 2064384 | bytes 8519680 | tf_op jit(solution)/shard_map/while/body/eval_jaxpr/reduce_sum | solution.py:53
  70.2 8.4 %pmax.7 = f32[2,512]{1,0:T(2,128)S(1)} all-reduce(f32[2,512]{1,0:T(2,128)S(1)} %reduce_max.9), channel_id=1, replica_groups=mesh['dp'=8,'comp'=4] {'comp'}, use_global_device_ids=true, to_apply=%region_5.6 | all-reduce | flops 1024 | bytes 8192 | tf_op jit(solution)/shard_map/pmax | solution.py:58
  79.5 5.8 %psum.7 = f32[2,512]{1,0:T(2,128)S(1)} all-reduce(f32[2,512]{1,0:T(2,128)S(1)} %exponential_reduce_fusion), channel_id=1, replica_groups=mesh['dp'=8,'comp'=4] {'comp'}, use_global_device_ids=true, to_apply=%region_7.8 | all-reduce | flops 1024 | bytes 8192 | tf_op jit(solution)/shard_map/psum | solution.py:60
  86.3 30.5 %while.26 = (s32[]{:T(128)}, f32[64,4096]{1,0:T(8,128)S(1)}, f32[64,64]{1,0:T(8,128)S(1)}, f32[64]{0:T(128)S(1)}, f32[2,64,512]{2,1,0:T(8,128)S(1)}, /*index=5*/f32[2,512,64]{1,0,2:T(2,128)S(1)}, s32[]{:T(128)}, s32[]{:T(128)}) while((s32[]{:T(128)}, f32[64,4096]{1,0:T(8,128)S(1)}, f32[64,64]{1,0:T(8,128)S(1)}, ...), condition=%wide.region_10.11_spmd.clone, body=%wide.region_8.10_spmd.clone.sunk | while | flops 1638441088 | bytes 20104304 | solution.py:78
  86.5 4.3 %broadcast_multiply_fusion.2 = f32[512,64,64]{0,2,1:T(8,128)} fusion(f32[512,64]{0,1:T(8,128)S(1)} %bitcast.79), kind=kLoop, calls=%fused_computation.8.clone.1 | loop fusion | flops 2097152 | bytes 8519680 | tf_op jit(solution)/shard_map/while/body/eval_jaxpr/mul | solution.py:66
  90.8 10.3 %convolution_add_fusion.4 = f32[64,4096]{1,0:T(8,128)S(1)} fusion(f32[512,4096]{0,1:T(8,128)} %bitcast.77, f32[64,4096]{1,0:T(8,128)S(1)} %get-tuple-element.277, pred[]{:T(512)S(6)} %compare.12, f32[2,64,512]{2,1,0:T(8,128)S(1)} %get-tuple-element.288, s32[]{:T(128)} %get-tuple-element.276), kind=kOutput, calls=%fused_computation.7.clone.1 | convolution fusion | flops 1611137024 | bytes 10616837 | tf_op jit(solution)/shard_map/while/body/eval_jaxpr/dot_general | solution.py:67
  101.7 4.3 %broadcast_multiply_fusion.2 = f32[512,64,64]{0,2,1:T(8,128)} fusion(f32[512,64]{0,1:T(8,128)S(1)} %bitcast.79), kind=kLoop, calls=%fused_computation.8.clone.1 | loop fusion | flops 2097152 | bytes 8519680 | tf_op jit(solution)/shard_map/while/body/eval_jaxpr/mul | solution.py:66
  106.1 10.3 %convolution_add_fusion.4 = f32[64,4096]{1,0:T(8,128)S(1)} fusion(f32[512,4096]{0,1:T(8,128)} %bitcast.77, f32[64,4096]{1,0:T(8,128)S(1)} %get-tuple-element.277, pred[]{:T(512)S(6)} %compare.12, f32[2,64,512]{2,1,0:T(8,128)S(1)} %get-tuple-element.288, s32[]{:T(128)} %get-tuple-element.276), kind=kOutput, calls=%fused_computation.7.clone.1 | convolution fusion | flops 1611137024 | bytes 10616837 | tf_op jit(solution)/shard_map/while/body/eval_jaxpr/dot_general | solution.py:67
  119.8 22.0 %all-reduce.2 = f32[64]{0:T(128)S(1)} all-reduce(f32[64]{0:T(128)S(1)} %get-tuple-element.72), channel_id=3, replica_groups=mesh['dp'=8,'comp'=4] {'dp'}, use_global_device_ids=true, to_apply=%region_12.13.clone | all-reduce | flops 64 | bytes 512
  142.0 33.9 %all-reduce.3 = (f32[64,64]{1,0:T(8,128)S(1)}, f32[64]{0:T(128)}) all-reduce(f32[64,64]{1,0:T(8,128)S(1)} %get-tuple-element.71, f32[64]{0:T(128)S(1)} %get-tuple-element.167), channel_id=2, replica_groups=mesh['dp'=8,'comp'=4] {'dp'}, use_global_device_ids=true, to_apply=%region_11.12.clone | all-reduce | flops 4160 | bytes 33280
  176.1 7.2 %reduce-scatter.2.cloned.1.call-done = f32[8,4096]{1,0:T(8,128)} async-done(((f32[64,4096]{1,0:T(8,128)}), f32[8,4096]{1,0:T(8,128)}) %reduce-scatter.2.cloned.1.call-update) | async-done | bytes 131088 | tf_op jit(solution)/shard_map/reduce_scatter | solution.py:81
  184.9 46.9 %custom-call.7 = f32[8,64,64]{2,1,0:T(8,128)S(1)} custom-call(f32[8,64,64]{2,1,0:T(8,128)S(1)} %fusion.11), custom_call_target="Cholesky" | custom-call | tf_op jit(solution)/shard_map/jit(cholesky)/cholesky | solution.py:30
  232.1 39.3 %custom-call.8 = f32[8,1,64,64]{2,3,1,0:T(8,128)S(1)} custom-call(f32[8,1,64,64]{3,2,1,0:T(8,128)S(1)} %select_bitcast_fusion), custom_call_target="InvertDiagBlocksLowerTriangular" | custom-call | tf_op jit(solution)/shard_map/triangular_solve | solution.py:31
  271.4 1.3 constant_dynamic-update-slice_fusion.7
  272.7 2.2 collective-permute-start
  274.9 4.2 %collective-permute-done = f32[8,64,64]{2,1,0:T(8,128)S(1)} collective-permute-done((f32[8,64,64]{2,1,0:T(8,128)S(1)}, f32[8,64,64]{2,1,0:T(8,128)S(1)}, u32[]{:S(2)}, u32[]{:S(2)}) %collective-permute-start) | collective-permute-done | bytes 131104 | tf_op jit(solution)/shard_map/ppermute | solution.py:16
  279.1 2.8 collective-permute-start.1
  281.9 8.9 %collective-permute-done.1 = f32[16,64,64]{2,1,0:T(8,128)S(1)} collective-permute-done((f32[16,64,64]{2,1,0:T(8,128)S(1)}, f32[16,64,64]{2,1,0:T(8,128)S(1)}, u32[]{:S(2)}, u32[]{:S(2)}) %collective-permute-start.1) | collective-permute-done | bytes 262176 | tf_op jit(solution)/shard_map/ppermute | solution.py:16
  291.0 1.9 collective-permute-start.2
  292.9 66.6 %all_gather.6 = f32[64,64]{1,0:T(8,128)S(1)} all-gather(f32[8,64]{1,0:T(8,128)S(1)} %get-tuple-element.165), channel_id=1, replica_groups=mesh['dp'=8,'comp'=4] {'dp'}, dimensions={0}, use_global_device_ids=true | all-gather | bytes 18432 | tf_op jit(solution)/shard_map/all_gather | solution.py:89
  361.6 1.1 constant_dynamic-update-slice_fusion.4
  366.0 3.2 constant_dynamic-slice_fusion.3
  (75 shorter events, 20.7 us)
Async XLA Ops:
  7.2 6.4 %copy-start = (f32[64,64]{1,0:T(8,128)S(1)}, f32[64,64]{1,0:T(8,128)}, u32[]{:S(2)}) copy-start(f32[64,64]{1,0:T(8,128)} %param.9) | copy-start | bytes 49156
  7.2 6.4 %copy-start.1 = (f32[64,64,64]{2,1,0:T(8,128)S(1)}, f32[64,64,64]{2,1,0:T(8,128)}, u32[]{:S(2)}) copy-start(f32[64,64,64]{2,1,0:T(8,128)} %param.10) | copy-start | bytes 3145732
  7.2 9.8 %copy-start.6 = (f32[64]{0:T(128)S(1)}, f32[64]{0:T(128)}, u32[]{:S(2)}) copy-start(f32[64]{0:T(128)} %param.11) | copy-start | bytes 772
  7.2 176.1 %reduce-scatter.2.cloned.1.call-start = ((), (), s32[]{:S(2)}) async-start(), calls=%async_computation.1 | async-start | bytes 1179648 | tf_op jit(solution)/shard_map/reduce_scatter | solution.py:81
  17.0 0.7 copy-start.3
  37.6 5.5 %copy-start.4 = (f32[2,512,64]{1,0,2:T(2,128)S(1)}, f32[2,512,64]{1,0,2:T(2,128)}, u32[]{:S(2)}) copy-start(f32[2,512,64]{1,0,2:T(2,128)} %copy-done.3) | copy-start | bytes 786436 | tf_op jit(solution)/shard_map/while
  43.1 0.7 copy-start.3
  63.7 5.5 %copy-start.4 = (f32[2,512,64]{1,0,2:T(2,128)S(1)}, f32[2,512,64]{1,0,2:T(2,128)}, u32[]{:S(2)}) copy-start(f32[2,512,64]{1,0,2:T(2,128)} %copy-done.3) | copy-start | bytes 786436 | tf_op jit(solution)/shard_map/while
  86.3 31.6 %copy-start.5 = (u32[32]{0:T(128)S(1)}, u32[32]{0:T(128)}, u32[]{:S(2)}) copy-start(u32[32]{0:T(128)} %constant.135) | copy-start | bytes 388
  116.8 1.0 copy-start.2
  272.7 6.4 %collective-permute-start = (f32[8,64,64]{2,1,0:T(8,128)S(1)}, f32[8,64,64]{2,1,0:T(8,128)S(1)}, u32[]{:S(2)}, u32[]{:S(2)}) collective-permute-start(f32[8,64,64]{2,1,0:T(8,128)S(1)} %get-tuple-element.172), channel_id=1, source_target_pairs={{0,28},{4,0},{8,4},{12,8},{16,12},{20,16},{24,20},{28,24},{1,29},{... | collective-permute-start | bytes 393224 | tf_op jit(solution)/shard_map/ppermute | solution.py:16
  279.1 11.7 %collective-permute-start.1 = (f32[16,64,64]{2,1,0:T(8,128)S(1)}, f32[16,64,64]{2,1,0:T(8,128)S(1)}, u32[]{:S(2)}, u32[]{:S(2)}) collective-permute-start(f32[16,64,64]{2,1,0:T(8,128)S(1)} %pad_maximum_fusion.1), channel_id=1, source_target_pairs={{0,24},{4,28},{8,0},{12,4},{16,8},{20,12},{24,16},{28,20},{1,25},{... | collective-permute-start | bytes 786440 | tf_op jit(solution)/shard_map/ppermute | solution.py:16
  291.0 70.6 %collective-permute-start.2 = (f32[32,64,64]{2,1,0:T(8,128)S(1)}, f32[32,64,64]{2,1,0:T(8,128)S(1)}, u32[]{:S(2)}, u32[]{:S(2)}) collective-permute-start(f32[32,64,64]{2,1,0:T(8,128)S(1)} %pad_maximum_fusion), channel_id=1, source_target_pairs={{0,16},{4,20},{8,24},{12,28},{16,0},{20,4},{24,8},{28,12},{1,17},{... | collective-permute-start | bytes 1572872 | tf_op jit(solution)/shard_map/ppermute | solution.py:16
Sparse Core Ops, SparseCore 0:
  118.0 65.2 reduce-scatter.1
